TPU v7x, 512 devices: a whole 4x4x16 slice. The times are simulated.
512 devices in a mesh: seq: 128 (over z, x, core), ch: 4 (over y).
Axes of the slice: x: 4, y: 4, z: 16, core: 2. Of those that a mesh axis runs over, the one named last changes fastest.
Arguments:
- values: float32 [32768, 1024], P('seq', 'ch'), may hold values from -6 to 6
- gates: float32 [32768, 1024], P('seq', 'ch'), may hold values from -6 to 6
- filter_taps: float32 [4096, 1024], P('seq', 'ch'), may hold values from -0.09375 to 0.09375
- skip: float32 [1024], P('ch'), may hold values from 0.5 to 2
- out_weight: bfloat16 [1024, 2048], P(None, 'ch'), may hold values from -0.1875 to 0.1875
Outputs:
- mixed: float32 [32768, 2048], P('seq', 'ch')
All inputs are finite; a program needn't handle non-finite values.
Results may differ from a plain program's by a relative error of at most 0.0058.
Values may be sent and summed in bfloat16 or wider, within the bound.
A program may use at most 64 MiB of HBM per device.

v0:
```python
import math

import jax
import jax.numpy as jnp
from jax import lax
from jax.sharding import Mesh
from jax.sharding import PartitionSpec as P

SEQ = ("seq_0", "seq_1", "seq_2")


HIGHEST = lax.Precision.HIGHEST


def in_order(parts, dim):
    parts = jnp.moveaxis(parts, 0, dim)
    shape = parts.shape
    return parts.reshape(*shape[:dim], shape[dim] * shape[dim + 1], *shape[dim + 2 :])


def gather_in_order(value, axes, order):
    parts = value
    for k in order:
        parts = lax.all_gather(parts, axes[k])
    done = order[::-1]
    back = [done.index(k) for k in range(len(axes))]
    parts = parts.transpose(*back, *range(len(axes), parts.ndim))
    return parts.reshape(-1, *value.shape)


def gather_axes(value, axes, order, dim):
    return in_order(gather_in_order(value, axes, order), dim)


def for_sending(value):

    def short(part):
        return part.astype(jnp.bfloat16) if part.dtype == jnp.float32 else part

    return jax.tree.map(short, value)


def split_length(length):
    leading = 1
    for factor in range(1, math.isqrt(length) + 1):
        if length % factor == 0:
            leading = factor
    return (leading, length // leading)


def phase_table(count_rows, count_cols, modulus):
    row_ids = jnp.arange(count_rows, dtype=jnp.int32)
    col_ids = jnp.arange(count_cols, dtype=jnp.int32)
    wrapped = row_ids[:, None] * col_ids[None, :] % modulus
    phases = 2.0 * math.pi / modulus * wrapped.astype(jnp.float32)
    return (jnp.cos(phases), jnp.sin(phases))


def complex_form(cosine, sine):
    upper = jnp.stack([cosine, -sine], axis=1)
    lower = jnp.stack([sine, cosine], axis=1)
    return jnp.stack([upper, lower], axis=0)


def transform_tables(length):
    rows_lead, rows_tail = split_length(length)
    cos_lead, sin_lead = phase_table(rows_lead, rows_lead, rows_lead)
    cos_tail, sin_tail = phase_table(rows_tail, rows_tail, rows_tail)
    cos_twist, sin_twist = phase_table(rows_lead, rows_tail, length)
    lead_table = jnp.stack([cos_lead, -sin_lead])
    tail_forward = complex_form(cos_tail, -sin_tail)
    tail_inverse = complex_form(cos_tail, sin_tail)
    return (
        lead_table,
        tail_forward,
        tail_inverse,
        cos_twist,
        sin_twist,
        rows_lead,
        rows_tail,
        length,
    )


def twist_rows(section, cosine, sine):
    real_part = section[0] * cosine[None] - section[1] * sine[None]
    imag_part = section[0] * sine[None] + section[1] * cosine[None]
    return jnp.stack([real_part, imag_part])


def forward_rows(rows, tables):
    lead_table, tail_forward, tail_inverse, cos_twist, sin_twist, rows_lead, rows_tail, length = (
        tables
    )
    signal = jnp.concatenate([rows, jnp.zeros_like(rows)], axis=1).reshape(
        rows.shape[0], rows_lead, rows_tail
    )
    section = jnp.einsum("pft,cts->pcfs", lead_table, signal, precision=HIGHEST)
    twisted = twist_rows(section, cos_twist, -sin_twist)
    return jnp.einsum("pgrs,rcfs->pcfg", tail_forward, twisted, precision=HIGHEST)


def inverse_rows(spectrum, tables):
    lead_table, tail_forward, tail_inverse, cos_twist, sin_twist, rows_lead, rows_tail, length = (
        tables
    )
    section = jnp.einsum("pgrs,rcfs->pcfg", tail_inverse, spectrum, precision=HIGHEST)
    twisted = twist_rows(section, cos_twist, sin_twist)
    signal = jnp.einsum("rft,rcfs->cts", lead_table, twisted, precision=HIGHEST) / length
    return signal.reshape(signal.shape[0], length)


def product(left, right):
    real_part = left[0] * right[0] - left[1] * right[1]
    imag_part = left[0] * right[1] + left[1] * right[0]
    return jnp.stack([real_part, imag_part])


def body(values, gates, filter_taps, skip, out_weight):
    block_rows, width = values.shape
    whole_filter = gather_axes(filter_taps, SEQ, (1, 0, 2), 0)
    devices = lax.axis_size(SEQ)
    narrow = width // devices
    whole_rows = lax.all_to_all(
        values.T.astype(jnp.bfloat16), SEQ, split_axis=0, concat_axis=1, tiled=True
    ).astype(jnp.float32)
    total_rows = whole_rows.shape[1]
    own_taps = lax.dynamic_slice_in_dim(whole_filter, lax.axis_index(SEQ) * narrow, narrow, 1).T
    used_taps = min(own_taps.shape[1], total_rows)
    taps_rows = jnp.concatenate(
        [own_taps, jnp.zeros((narrow, total_rows - used_taps), jnp.float32)], axis=1
    )
    row_tables = transform_tables(2 * total_rows)
    spectrum = product(forward_rows(whole_rows, row_tables), forward_rows(taps_rows, row_tables))
    convolved_rows = inverse_rows(spectrum, row_tables)[:, :total_rows]
    convolved = (
        lax.all_to_all(for_sending(convolved_rows), SEQ, split_axis=1, concat_axis=0, tiled=True)
        .astype(convolved_rows.dtype)
        .T
    )
    hidden = (gates * (convolved + skip[None, :] * values)).astype(jnp.bfloat16)
    return jnp.dot(
        lax.all_gather(hidden, "ch", axis=1, tiled=True),
        out_weight,
        preferred_element_type=jnp.float32,
    )


def solution(mesh):
    torus = Mesh(
        mesh.devices.reshape(16, 4, 2, mesh.shape["ch"]), ("seq_0", "seq_1", "seq_2", "ch")
    )
    in_specs = (P(SEQ, "ch"), P(SEQ, "ch"), P(SEQ, "ch"), P("ch"), P(None, "ch"))
    out_specs = P(SEQ, "ch")
    return jax.shard_map(body, mesh=torus, in_specs=in_specs, out_specs=out_specs, check_vma=False)
```

profile of v0, /device:TPU:1, one launch (start us, length us, event | category | flops | bytes accessed | tf_op | source)
XLA Modules:
  0.0 196.1 jit_solution(9870822380888516193)
XLA Ops:
  6.5 12.6 %all-gather = f32[128,256]{1,0:T(8,128)} all-gather(f32[32,256]{1,0:T(8,128)} %param.7), channel_id=2, replica_groups=mesh['seq_0'=16,'seq_1'=4,'seq_2'=2,'ch'=4] {'seq_1'}, dimensions={0}, use_global_device_ids=true | all-gather | bytes 163840 | tf_op jit(solution)/shard_map/all_gather | solution.py:24
  19.2 0.0 all-gather.6.cloned.1.call-update
  19.2 0.0 all-gather.8.cloned.1.call-start
  19.2 69.0 %all-gather.6.cloned.1.call-done = f32[64,32,256]{2,1,0:T(8,128)} async-done(((f32[4,32,256]{2,1,0:T(8,128)}), f32[64,32,256]{2,1,0:T(8,128)}) %all-gather.6.cloned.1.call-update) | async-done | bytes 2097168 | tf_op jit(solution)/shard_map/all_gather | solution.py:24
  88.2 0.0 all-gather.8.cloned.1.call-update
  88.3 1.0 convert_bitcast_fusion.1
  89.2 0.1 copy.33
  89.3 0.7 all_to_all.20
  90.0 21.4 %all-to-all-start = ((bf16[128,2,256]{2,1,0:T(2,128)(2,1)}), bf16[128,2,256]{2,1,0:T(2,128)(2,1)S(1)}, u32[]{:S(2)}, u32[]{:S(2)}) async-start(bf16[128,2,256]{2,1,0:T(2,128)(2,1)} %all_to_all.20), calls=%async_computation | async-start | bytes 262144 | tf_op jit(solution)/shard_map/all_to_all | solution.py:124
  111.4 0.7 pad.16.clone
  112.2 0.7 pad.15.clone
  112.9 1.0 fusion.46
  113.9 1.0 sine_negate_fusion
  115.0 1.7 fusion.42
  116.6 1.8 fusion.43
  118.4 1.0 fusion.40
  119.5 1.5 fusion.17
  121.0 6.5 %all-to-all-done = bf16[128,2,256]{2,1,0:T(2,128)(2,1)S(1)} async-done(((bf16[128,2,256]{2,1,0:T(2,128)(2,1)}), bf16[128,2,256]{2,1,0:T(2,128)(2,1)S(1)}, u32[]{:S(2)}, u32[]{:S(2)}) %all-to-all-start) | async-done | bytes 131104 | tf_op jit(solution)/shard_map/all_to_all | solution.py:124
  127.5 0.2 concatenate.6
  127.6 1.7 convolution_bitcast_fusion.4
  129.3 2.5 %copy.36 = f32[16,4,2,32,256]{4,3,2,1,0:T(8,128)S(1)} copy(f32[16,4,2,32,256]{4,3,1,0,2:T(8,128)} %bitcast.109) | data formatting | bytes 8388608 | tf_op jit(solution)/shard_map/transpose | solution.py:27
  131.8 0.6 dynamic-slice_bitcast_fusion
  132.5 0.6 copy.37
  133.1 1.4 maximum_maximum_fusion
  134.5 2.8 %convolution_bitcast_fusion.2 = f32[2,2,256,256]{2,3,0,1:T(8,128)S(1)} fusion(f32[1,2,256,256]{3,1,2,0:T(2,128)S(1)} %bitcast.111, f32[1,256,256]{2,1,0:T(8,128)S(1)} %get-tuple-element.21, f32[1,256,256]{2,1,0:T(8,128)} %copy-done.3), kind=kOutput, calls=%fused_computation.3 | convolution fusion | flops 805437440 | bytes 2097152 | tf_op jit(solution)/shard_map/pft,cts->pcfs/dot_general | solution.py:98
  137.3 1.6 multiply_subtract_fusion.3
  139.0 0.0 copy-start.6
  139.0 3.6 %convolution_bitcast_fusion.3 = f32[2,2,256,256]{3,2,0,1:T(8,128)S(1)} fusion(f32[1,2,256,256]{2,3,0,1:T(8,128)S(1)} %get-tuple-element.10, f32[1,2,256,256]{2,3,0,1:T(8,128)S(1)} %get-tuple-element.9, f32[1,256,2,256]{3,1,2,0:T(8,128)S(1)} %copy-done.1, f32[1,256,2,256]{3,1,2,0:T(8,128)S(1)} %copy-done.2), kind=kOutput, calls=%fused_computation.4 | convolution fusion | flops 1611137024 | bytes 3145728 | tf_op jit(solution)/shard_map/pgrs,rcfs->pcfg/dot_general | solution.py:100
  142.6 3.8 %convolution_bitcast_fusion.1 = f32[2,2,256,256]{3,2,0,1:T(8,128)S(1)} fusion(f32[1,2,256,256]{2,3,0,1:T(8,128)S(1)} %get-tuple-element.17, f32[1,2,256,256]{2,3,0,1:T(8,128)S(1)} %get-tuple-element.18, f32[1,256,2,256]{3,1,2,0:T(8,128)S(1)} %copy-done.1, f32[1,256,2,256]{3,1,2,0:T(8,128)S(1)} %copy-done.2), kind=kOutput, calls=%fused_computation.2 | convolution fusion | flops 1611137024 | bytes 3145728 | tf_op jit(solution)/shard_map/pgrs,rcfs->pcfg/dot_general | solution.py:100
  146.4 0.1 multiply_subtract_fusion.1
  146.5 0.0 copy-start.9
  146.5 0.0 copy-start.10
  146.5 1.9 convolution_bitcast_fusion
  148.5 0.0 copy-start.11
  148.5 0.1 multiply_subtract_fusion
  148.6 1.0 fusion.2
  149.6 0.1 copy.41
  149.8 0.3 copy.65
  150.0 0.7 slice.65
  150.8 9.6 %all-to-all-start.1 = ((bf16[2,128,256]{2,0,1:T(2,128)(2,1)}), bf16[2,128,256]{2,0,1:T(2,128)(2,1)S(1)}, u32[]{:S(2)}, u32[]{:S(2)}) async-start(bf16[2,128,256]{2,0,1:T(2,128)(2,1)} %bitcast.38), calls=%async_computation.1 | async-start | bytes 262144 | tf_op jit(solution)/shard_map/all_to_all | solution.py:137
  160.4 0.1 copy.43
  160.6 0.1 copy.44
  160.7 15.7 %all-to-all-done.1 = bf16[2,128,256]{2,0,1:T(2,128)(2,1)S(1)} async-done(((bf16[2,128,256]{2,0,1:T(2,128)(2,1)}), bf16[2,128,256]{2,0,1:T(2,128)(2,1)S(1)}, u32[]{:S(2)}, u32[]{:S(2)}) %all-to-all-start.1) | async-done | bytes 131104 | tf_op jit(solution)/shard_map/all_to_all | solution.py:137
  176.4 0.1 convert_bitcast_fusion
  176.5 0.2 reshape.223
  176.7 0.1 fusion.30
  176.8 11.2 %all_gather.27 = bf16[256,1024]{0,1:T(8,128)(2,1)S(1)} all-gather(bf16[256,256]{0,1:T(8,128)(2,1)S(1)} %fusion.30), channel_id=1, replica_groups=mesh['seq_0'=16,'seq_1'=4,'seq_2'=2,'ch'=4] {'ch'}, dimensions={1}, use_global_device_ids=true | all-gather | bytes 655360 | tf_op jit(solution)/shard_map/all_gather | solution.py:143
  188.0 1.3 fusion.53
  (24 shorter events, 0.1 us)
Async XLA Ops:
  6.5 181.5 %copy-start = (bf16[1024,512]{1,0:T(8,128)(2,1)S(1)}, bf16[1024,512]{1,0:T(8,128)(2,1)}, u32[]{:S(2)}) copy-start(bf16[1024,512]{1,0:T(8,128)(2,1)} %param.9) | copy-start | bytes 3145732
  6.5 81.7 %all-gather.6.cloned.1.call-start = ((), (), s32[]{:S(2)}) async-start(), calls=%async_computation.2 | async-start | bytes 2228224 | tf_op jit(solution)/shard_map/all_gather | solution.py:24
  19.2 110.1 %all-gather.8.cloned.1.call-start = ((), (), s32[]{:S(2)}) async-start(), calls=%async_computation.3 | async-start | bytes 6291456 | tf_op jit(solution)/shard_map/all_gather | solution.py:24
  90.0 37.4 %all-to-all-start = ((bf16[128,2,256]{2,1,0:T(2,128)(2,1)}), bf16[128,2,256]{2,1,0:T(2,128)(2,1)S(1)}, u32[]{:S(2)}, u32[]{:S(2)}) async-start(bf16[128,2,256]{2,1,0:T(2,128)(2,1)} %all_to_all.20), calls=%async_computation | async-start | bytes 262144 | tf_op jit(solution)/shard_map/all_to_all | solution.py:124
  115.0 16.9 %copy-start.3 = (f32[1,256,256]{2,1,0:T(8,128)}, f32[1,256,256]{2,1,0:T(8,128)S(1)}, u32[]{:S(2)}) copy-start(f32[1,256,256]{2,1,0:T(8,128)S(1)} %get-tuple-element.22) | copy-start | bytes 786436
  133.1 5.9 %copy-start.1 = (f32[1,256,2,256]{3,1,2,0:T(8,128)S(1)}, f32[1,256,2,256]{3,1,2,0:T(8,128)}, u32[]{:S(2)}) copy-start(f32[1,256,2,256]{3,1,2,0:T(8,128)} %get-tuple-element.14) | copy-start | bytes 1572868
  133.1 5.9 %copy-start.2 = (f32[1,256,2,256]{3,1,2,0:T(8,128)S(1)}, f32[1,256,2,256]{3,1,2,0:T(8,128)}, u32[]{:S(2)}) copy-start(f32[1,256,2,256]{3,1,2,0:T(8,128)} %get-tuple-element.19) | copy-start | bytes 1572868
  139.0 7.5 %copy-start.6 = (f32[1,256,2,256]{3,1,2,0:T(8,128)S(1)}, f32[1,256,2,256]{3,1,2,0:T(8,128)}, u32[]{:S(2)}) copy-start(f32[1,256,2,256]{3,1,2,0:T(8,128)} %get-tuple-element.13) | copy-start | bytes 1572868
  139.0 7.5 %copy-start.7 = (f32[1,256,2,256]{3,1,2,0:T(8,128)S(1)}, f32[1,256,2,256]{3,1,2,0:T(8,128)}, u32[]{:S(2)}) copy-start(f32[1,256,2,256]{3,1,2,0:T(8,128)} %get-tuple-element.20) | copy-start | bytes 1572868
  142.5 5.9 %copy-start.5 = (f32[256,256]{0,1:T(8,128)S(1)}, f32[256,256]{0,1:T(8,128)}, u32[]{:S(2)}) copy-start(f32[256,256]{0,1:T(8,128)} %get-tuple-element.23) | copy-start | bytes 786436
  142.6 5.9 %copy-start.8 = (f32[256,256]{0,1:T(8,128)S(1)}, f32[256,256]{0,1:T(8,128)}, u32[]{:S(2)}) copy-start(f32[256,256]{0,1:T(8,128)} %fusion.42) | copy-start | bytes 786436
  146.3 2.3 %copy-start.4 = (f32[1,256,256]{2,1,0:T(8,128)S(1)}, f32[1,256,256]{2,1,0:T(8,128)}, u32[]{:S(2)}) copy-start(f32[1,256,256]{2,1,0:T(8,128)} %copy-done.3) | copy-start | bytes 786436
  146.5 13.9 %copy-start.9 = (f32[256,256]{1,0:T(8,128)S(1)}, f32[256,256]{1,0:T(8,128)}, u32[]{:S(2)}) copy-start(f32[256,256]{1,0:T(8,128)} %param.5) | copy-start | bytes 786436
  146.5 14.0 %copy-start.10 = (f32[256,256]{1,0:T(8,128)S(1)}, f32[256,256]{1,0:T(8,128)}, u32[]{:S(2)}) copy-start(f32[256,256]{1,0:T(8,128)} %param.6) | copy-start | bytes 786436
  148.5 28.2 %copy-start.11 = (f32[256]{0:T(256)S(1)}, f32[256]{0:T(256)}, u32[]{:S(2)}) copy-start(f32[256]{0:T(256)} %param.8) | copy-start | bytes 3076
  150.8 25.6 %all-to-all-start.1 = ((bf16[2,128,256]{2,0,1:T(2,128)(2,1)}), bf16[2,128,256]{2,0,1:T(2,128)(2,1)S(1)}, u32[]{:S(2)}, u32[]{:S(2)}) async-start(bf16[2,128,256]{2,0,1:T(2,128)(2,1)} %bitcast.38), calls=%async_computation.1 | async-start | bytes 262144 | tf_op jit(solution)/shard_map/all_to_all | solution.py:137
Sparse Core Ops, SparseCore 0:
  19.3 68.8 all-gather.5
  90.3 31.6 all-gather.7
where the time goes:
time: 198 us; the launch traced here: 196 us
  waiting for transfers between devices  91.2 us (46%)
  starting transfers between devices  31 us (16%)
  blocking collectives  23.8 us (12%)
  matrix products  15.9 us (8%)
  between operations  13.8 us (7%)
  other arithmetic  12.5 us (6%)
  local copies, waits for them, and re-layouts  7.84 us (4%)
    all_gather x2, waiting for transfers between devices, gather_in_order(): parts = lax.all_gather(parts, axes[k])  69 us
    all_to_all x1, starting transfers between devices, body(): lax.all_to_all(values.T.astype(jnp.bfloat16), SEQ, split_axis=0, concat_a...  21.4 us
    all_to_all x1, waiting for transfers between devices, body(): lax.all_to_all(for_sending(convolved_rows), SEQ, split_axis=1, concat_axi...  15.7 us
    all_gather x1, blocking collectives, gather_in_order(): parts = lax.all_gather(parts, axes[k])  12.6 us
    all_gather x1, blocking collectives, body(): lax.all_gather(hidden, 'ch', axis=1, tiled=True)  11.2 us
    all_to_all x1, starting transfers between devices, body(): lax.all_to_all(for_sending(convolved_rows), SEQ, split_axis=1, concat_axi...  9.61 us
    dot_general x2, matrix products, forward_rows(): jnp.einsum('pgrs,rcfs->pcfg', tail_forward, twisted, precision=HIGHEST)  7.32 us
    all_to_all x1, waiting for transfers between devices, body(): lax.all_to_all(values.T.astype(jnp.bfloat16), SEQ, split_axis=0, concat_a...  6.5 us
  transfers between devices with their start and end apart: 4, of which 3 were waited for; matrix products, arithmetic and copies ran while one was open for 6% of the time, Pallas kernels for 0%

commit v1 on v0

v1 whole, which is shorter than its diff:
```python
import functools

import jax
import jax.numpy as jnp
from jax import lax
from jax.experimental import pallas as pl
from jax.experimental.pallas import tpu as pltpu
from jax.sharding import Mesh
from jax.sharding import PartitionSpec as P

MESH = pl.DeviceIdType.MESH
F32 = jnp.float32
BF16 = jnp.bfloat16
VMEM = pltpu.VMEM
ANY = pl.BlockSpec(memory_space=pl.ANY)
NZ, NW = 16, 8


def each(low, high, step):
    def run(k, _):
        step(k)
        return 0

    lax.fori_loop(low, high, run, 0)


def greet(axis, size):
    me = lax.axis_index(axis)
    barrier = pltpu.get_barrier_semaphore()
    for k in range(1, size):
        pl.semaphore_signal(barrier, inc=1, device_id={axis: lax.rem(me + k, size)}, device_id_type=MESH)


def wait_for(count):
    pl.semaphore_wait(pltpu.get_barrier_semaphore(), count)


def spread_kernel(values_hbm, taps_hbm, out, values, taps, send_values, send_taps, got_taps, local_sem, send_sem, recv_sem):
    me = lax.axis_index("w")
    greet("w", NW)
    loads = [
        pltpu.make_async_copy(taps_hbm, taps, local_sem.at[0]),
        pltpu.make_async_copy(values_hbm, values, local_sem.at[1]),
    ]
    for load in loads:
        load.start()
    loads[0].wait()
    own = jnp.concatenate([taps[...], jnp.zeros((96, 256), F32)], axis=0)
    own = pltpu.roll(own.T, 32 * lax.rem(me, 4), 1)
    send_taps[...] = own.astype(BF16).reshape(NW, NZ, 2, 128)
    loads[1].wait()
    for half in range(2):
        turned = values[half * 128:(half + 1) * 128, :].T
        send_values[half] = turned.astype(BF16).reshape(NW, NZ, 2, 128)
    wait_for(NW - 1)

    def taps_to(k):
        peer = lax.rem(me + k, NW)
        return pltpu.make_async_remote_copy(
            src_ref=send_taps.at[peer], dst_ref=got_taps.at[k], send_sem=send_sem.at[0, k],
            recv_sem=recv_sem.at[0, k], device_id={"w": peer}, device_id_type=MESH)

    def values_to(k):
        peer = lax.rem(me + k, NW)
        return pltpu.make_async_remote_copy(
            src_ref=send_values.at[:, peer], dst_ref=out.at[pl.ds(2 * me, 2)], send_sem=send_sem.at[1, k],
            recv_sem=recv_sem.at[1, k], device_id={"w": peer}, device_id_type=MESH)

    order = (4, 3, 5, 2, 6, 1, 7)
    for k in order:
        taps_to(k).start()
        values_to(k).start()
    out[pl.ds(2 * me, 2)] = send_values[:, me]
    got_taps[0] = send_taps[me]
    for k in order:
        taps_to(k).wait()
    for half in range(2):
        from_w = lambda w: got_taps[lax.rem(me + NW - w, NW)]
        w = 4 * half
        out[16 + half] = (from_w(w) + from_w(w + 1)) + (from_w(w + 2) + from_w(w + 3))
    for k in order:
        values_to(k).wait()


def convolve_kernel(rows_hbm, back, rows, got, got_taps, blocks, lags, toeplitz, total, results, local_sem, send_sem, recv_sem):
    me = lax.axis_index("z")
    greet("z", NZ)
    load = pltpu.make_async_copy(rows_hbm, rows, local_sem)
    load.start()
    load.wait()
    odd, high = lax.rem(me, 2), me // 2
    got[pl.ds(16 * odd, 16), high] = rows[0:16, me]
    got_taps[me] = rows[16:18, me]
    wait_for(NZ - 1)

    def taps_to(k):
        peer = lax.rem(me + k, NZ)
        return pltpu.make_async_remote_copy(
            src_ref=rows.at[pl.ds(16, 2), peer], dst_ref=got_taps.at[me], send_sem=send_sem.at[0, k],
            recv_sem=recv_sem.at[0, k], device_id={"z": peer}, device_id_type=MESH)

    def values_to(k):
        peer = lax.rem(me + k, NZ)
        return pltpu.make_async_remote_copy(
            src_ref=rows.at[pl.ds(0, 16), peer], dst_ref=got.at[pl.ds(16 * odd, 16), high], send_sem=send_sem.at[1, k],
            recv_sem=recv_sem.at[1, k], device_id={"z": peer}, device_id_type=MESH)

    def back_to(k):
        peer = lax.rem(me + k, NZ)
        return pltpu.make_async_remote_copy(
            src_ref=results.at[pl.ds(16 * lax.rem(peer, 2), 16), peer // 2], dst_ref=back.at[:, me],
            send_sem=send_sem.at[2, k], recv_sem=recv_sem.at[2, k], device_id={"z": peer}, device_id_type=MESH)

    order = (8, 7, 9, 6, 10, 5, 11, 4, 12, 3, 13, 2, 14, 1, 15)
    for k in order:
        taps_to(k).start()
    for k in order:
        values_to(k).start()
    for k in order:
        taps_to(k).wait()
    each(0, NZ, lambda z: lags.__setitem__(pl.ds(pl.multiple_of(4 * z, 4), 4), got_taps[z].astype(F32).reshape(4, 128)))

    row = lax.broadcasted_iota(jnp.int32, (128, 128), 0)
    col = lax.broadcasted_iota(jnp.int32, (128, 128), 1)
    after = col >= row
    zero = jnp.zeros((128, 128), F32)

    def turned_rows(j, c):
        line = lags[pl.ds(2 * j + c, 1), :]
        return pltpu.roll(jnp.broadcast_to(line, (128, 128)), 0, 1, stride=1, stride_axis=0)

    for c in range(2):
        lanes = slice(c * 128, (c + 1) * 128)
        first = turned_rows(0, c)
        toeplitz[0, :, lanes] = jnp.where(after, first, zero).astype(BF16)

        def place(j, before):
            current = turned_rows(j, c)
            toeplitz[j, :, lanes] = jnp.where(after, current, before).astype(BF16)
            return current

        last = lax.fori_loop(1, 32, place, first)
        toeplitz[32, :, lanes] = jnp.where(after, zero, last).astype(BF16)

    for k in order:
        values_to(k).wait()

    def unpack(l):
        x = got[l].astype(F32).reshape(16, 128)
        blocks[32 + l] = x.astype(BF16)
        blocks[l] = jnp.concatenate([jnp.zeros((2, 128), F32), x[:14]], axis=0).astype(BF16)

    each(0, 32, unpack)

    def left(j):
        return blocks[pl.ds(32 - j, 32)].reshape(512, 128)

    total[...] = jnp.dot(left(32), toeplitz[32], preferred_element_type=F32)

    def add(k):
        pair = jnp.concatenate([left(2 * k), left(2 * k + 1)], axis=1)
        total[...] += jnp.dot(pair, toeplitz[pl.ds(2 * k, 2)].reshape(256, 256), preferred_element_type=F32)

    each(0, 16, add)

    even = lax.rem(lax.broadcasted_iota(jnp.int32, (16, 128), 0), 2) == 0

    def pick(l):
        both = total[pl.ds(pl.multiple_of(16 * l, 16), 16), :]
        results[l] = jnp.where(even, both[:, :128], both[:, 128:]).astype(BF16).reshape(8, 2, 128)

    each(0, 32, pick)
    for k in order:
        back_to(k).start()
    back[:, me] = results[pl.ds(16 * odd, 16), high]
    for k in order:
        back_to(k).wait()


def mix_kernel(
    back_hbm, values_hbm, gates_hbm, skip_ref, weight_hbm, out_ref,
    back, values, gates, weight, got, hidden, gathered, local_sem, send_sem, recv_sem, side_send, side_recv,
):
    me = lax.axis_index("w")
    my_ch = lax.axis_index("ch")
    greet("w", NW)
    greet("ch", 4)
    loads = [
        pltpu.make_async_copy(source, target, local_sem.at[k])
        for k, (source, target) in enumerate(
            ((back_hbm, back), (values_hbm, values), (gates_hbm, gates), (weight_hbm, weight))
        )
    ]
    for load in loads:
        load.start()
    loads[0].wait()
    got[:, me] = back[pl.ds(2 * me, 2)]
    wait_for(NW - 1 + 3)

    def part_to(k):
        peer = lax.rem(me + k, NW)
        return pltpu.make_async_remote_copy(
            src_ref=back.at[pl.ds(2 * peer, 2)], dst_ref=got.at[:, me], send_sem=send_sem.at[k],
            recv_sem=recv_sem.at[k], device_id={"w": peer}, device_id_type=MESH)

    order = (4, 3, 5, 2, 6, 1, 7)
    for k in order:
        part_to(k).start()
    loads[1].wait()
    loads[2].wait()
    for k in order:
        part_to(k).wait()

    for half in range(2):
        rows = slice(half * 128, (half + 1) * 128)
        convolved = got[half].astype(F32).reshape(256, 128).T
        hidden[rows, :] = (gates[rows, :] * (convolved + skip_ref[...] * values[rows, :])).astype(BF16)

    def side_to(k):
        return pltpu.make_async_remote_copy(
            src_ref=hidden, dst_ref=gathered.at[k - 1], send_sem=side_send.at[k - 1],
            recv_sem=side_recv.at[k - 1], device_id={"ch": lax.rem(my_ch + k, 4)}, device_id_type=MESH)

    for k in (2, 1, 3):
        side_to(k).start()
    loads[3].wait()

    def part(block, channel):
        rows = pl.ds(pl.multiple_of(channel * 256, 256), 256)
        return jnp.dot(block, weight[rows, :], preferred_element_type=F32)

    out_ref[...] = part(hidden[...], my_ch)
    for k in (1, 3, 2):
        side_to(k).wait()
        out_ref[...] += part(gathered[k - 1], lax.rem(my_ch + 4 - k, 4))


def body(values, gates, filter_taps, skip, out_weight):
    dma = pltpu.SemaphoreType.DMA
    vmem = pl.BlockSpec(memory_space=VMEM)
    spread = pl.pallas_call(
        spread_kernel,
        out_shape=jax.ShapeDtypeStruct((18, NZ, 2, 128), BF16),
        in_specs=[ANY, ANY],
        out_specs=vmem,
        scratch_shapes=[
            VMEM((256, 256), F32), VMEM((32, 256), F32), VMEM((2, NW, NZ, 2, 128), BF16),
            VMEM((NW, NZ, 2, 128), BF16), VMEM((NW, NZ, 2, 128), BF16), dma((2,)), dma((2, NW)), dma((2, NW)),
        ],
        compiler_params=pltpu.CompilerParams(collective_id=0, has_side_effects=True),
    )(values, filter_taps)
    back = pl.pallas_call(
        convolve_kernel,
        out_shape=jax.ShapeDtypeStruct((16, NZ, 2, 128), BF16),
        in_specs=[ANY],
        out_specs=vmem,
        scratch_shapes=[
            VMEM((18, NZ, 2, 128), BF16), VMEM((32, 8, 2, 128), BF16), VMEM((NZ, 2, 2, 128), BF16),
            VMEM((64, 16, 128), BF16), VMEM((64, 128), F32), VMEM((33, 128, 256), BF16), VMEM((512, 256), F32),
            VMEM((32, 8, 2, 128), BF16), dma, dma((3, NZ)), dma((3, NZ)),
        ],
        compiler_params=pltpu.CompilerParams(collective_id=1, has_side_effects=True),
    )(spread)
    return pl.pallas_call(
        mix_kernel,
        out_shape=jax.ShapeDtypeStruct((256, 512), F32),
        in_specs=[ANY, ANY, ANY, vmem, ANY],
        out_specs=vmem,
        scratch_shapes=[
            VMEM((16, NZ, 2, 128), BF16), VMEM((256, 256), F32), VMEM((256, 256), F32), VMEM((1024, 512), BF16),
            VMEM((2, NW, NZ, 2, 128), BF16), VMEM((256, 256), BF16), VMEM((3, 256, 256), BF16),
            dma((4,)), dma((NW,)), dma((NW,)), dma((3,)), dma((3,)),
        ],
        compiler_params=pltpu.CompilerParams(collective_id=2, has_side_effects=True),
    )(back, values, gates, skip.reshape(1, 256), out_weight)


def solution(mesh):
    torus = Mesh(mesh.devices.reshape(NZ, NW, 4), ("z", "w", "ch"))
    tokens = ("z", "w")
    return jax.shard_map(
        body,
        mesh=torus,
        in_specs=(P(tokens, "ch"), P(tokens, "ch"), P(tokens, "ch"), P("ch"), P(None, "ch")),
        out_specs=P(tokens, "ch"),
        check_vma=False,
    )
```

time: 198 us -> 71.8 us (0.36)
  waiting for transfers between devices: 91.2 us -> 0 us
  Pallas kernels: 0 us -> 69.7 us
  starting transfers between devices: 31 us -> 0 us
  blocking collectives: 23.8 us -> 0 us
  matrix products: 15.9 us -> 0 us
  between operations: 13.8 us -> 0.02 us
  other arithmetic: 12.5 us -> 0 us
  local copies, waits for them, and re-layouts: 7.84 us -> 1.87 us
    pallas_call x0 -> x3, Pallas kernels: none -> 69.7 us  [the longest x1 33.9 us: body(): pl.pallas_call(convolve_kernel, out_shape=jax.ShapeDtypeStruct((16, NZ, 2...]
    all_gather x2 -> x0, waiting for transfers between devices: 69 us -> none  [gather_in_order(): parts = lax.all_gather(parts, axes[k])]
    all_to_all x2 -> x0, starting transfers between devices: 31 us -> none  [the longest x1 21.4 us: body(): lax.all_to_all(values.T.astype(jnp.bfloat16), SEQ, split_axis=0, concat_a...]
    all_gather x2 -> x0, blocking collectives: 23.8 us -> none  [the longest x1 12.6 us: gather_in_order(): parts = lax.all_gather(parts, axes[k])]
    all_to_all x2 -> x0, waiting for transfers between devices: 22.2 us -> none  [the longest x1 15.7 us: body(): lax.all_to_all(for_sending(convolved_rows), SEQ, split_axis=1, concat_axi...]
    dot_general x7 -> x0, matrix products: 15.9 us -> none  [the longest x2 7.32 us: forward_rows(): jnp.einsum('pgrs,rcfs->pcfg', tail_forward, twisted, precision=HIGHEST)]
    transpose x4 -> x0, local copies, waits for them, and re-layouts: 3.91 us -> none  [the longest x1 2.5 us: gather_in_order(): parts = parts.transpose(*back, *range(len(axes), parts.ndim))]
    sin x2 -> x0, other arithmetic: 2.72 us -> none  [phase_table(): return (jnp.cos(phases), jnp.sin(phases))]
  transfers between devices with their start and end apart: 4 -> 0, of which waited for: 3 -> 0; matrix products, arithmetic and copies ran while one was open for 6% -> 0% of each run, Pallas kernels for 0% -> 0%
where the time goes in v1:
time: 71.8 us; the launch traced here: 71.5 us
  Pallas kernels  69.7 us (97%)
  local copies, waits for them, and re-layouts  1.87 us (3%)
    pallas_call x1, Pallas kernels, body(): pl.pallas_call(convolve_kernel, out_shape=jax.ShapeDtypeStruct((16, NZ, 2...  33.9 us
    pallas_call x1, Pallas kernels, body(): pl.pallas_call(mix_kernel, out_shape=jax.ShapeDtypeStruct((256, 512), F32...  21.5 us
    pallas_call x1, Pallas kernels, body(): pl.pallas_call(spread_kernel, out_shape=jax.ShapeDtypeStruct((18, NZ, 2,...  14.2 us
    unnamed x1, local copies, waits for them, and re-layouts  1.87 us

profile of v1, /device:TPU:1, one launch (start us, length us, event | category | flops | bytes accessed | tf_op | source)
XLA Modules:
  0.0 71.5 jit_solution(15720060659863664299)
XLA Ops:
  0.0 14.2 %shard_map.55.rows_hbm = bf16[18,16,2,128]{3,2,1,0:T(2,128)(2,1)} custom-call(f32[256,256]{1,0:T(8,128)} %values_hbm.3, f32[32,256]{1,0:T(8,128)} %taps_hbm.1), custom_call_target="tpu_custom_call" | custom-call | tf_op jit(solution)/shard_map/pallas_call | solution.py:241
  14.2 33.9 %shard_map.56.back_hbm = bf16[16,16,2,128]{3,2,1,0:T(2,128)(2,1)} custom-call(bf16[18,16,2,128]{3,2,1,0:T(2,128)(2,1)} %shard_map.55.rows_hbm), custom_call_target="tpu_custom_call" | custom-call | tf_op jit(solution)/shard_map/pallas_call | solution.py:252
  48.1 21.5 %shard_map.57 = f32[256,512]{1,0:T(8,128)} custom-call(bf16[16,16,2,128]{3,2,1,0:T(2,128)(2,1)} %shard_map.56.back_hbm, f32[256,256]{1,0:T(8,128)} %values_hbm.3, f32[256,256]{1,0:T(8,128)} %gates_hbm.1, f32[1,256]{1,0:T(1,128)} %bitcast.1, bf16[1024,512]{1,0:T(8,128)(2,1)} %weight_hbm.1), custom_call_target="tpu_custom_call" | custom-call | tf_op jit(solution)/shard_map/pallas_call | solution.py:264
  69.7 1.9 %copy.7 = f32[256,512]{1,0:T(8,128)} copy(f32[256,512]{1,0:T(8,128)} %shard_map.57) | data formatting | bytes 1048576

commit v2 on v1

--- a/solution.py
+++ b/solution.py
@@ -82,12 +82,9 @@
         values_to(k).wait()
 
 
-def convolve_kernel(rows_hbm, back, rows, got, got_taps, blocks, lags, toeplitz, total, results, local_sem, send_sem, recv_sem):
+def convolve_kernel(rows, back, got, got_taps, blocks, lags, toeplitz, results, send_sem, recv_sem):
     me = lax.axis_index("z")
     greet("z", NZ)
-    load = pltpu.make_async_copy(rows_hbm, rows, local_sem)
-    load.start()
-    load.wait()
     odd, high = lax.rem(me, 2), me // 2
     got[pl.ds(16 * odd, 16), high] = rows[0:16, me]
     got_taps[me] = rows[16:18, me]
@@ -118,58 +115,50 @@
         values_to(k).start()
     for k in order:
         taps_to(k).wait()
-    each(0, NZ, lambda z: lags.__setitem__(pl.ds(pl.multiple_of(4 * z, 4), 4), got_taps[z].astype(F32).reshape(4, 128)))
+    lags[0:2] = jnp.zeros((2, 128), F32)
+    lags[66:68] = jnp.zeros((2, 128), F32)
+    for z in range(NZ):
+        lags[2 + 4 * z:6 + 4 * z] = got_taps[z].astype(F32).reshape(4, 128)
 
     row = lax.broadcasted_iota(jnp.int32, (128, 128), 0)
     col = lax.broadcasted_iota(jnp.int32, (128, 128), 1)
-    after = col >= row
-    zero = jnp.zeros((128, 128), F32)
-
-    def turned_rows(j, c):
-        line = lags[pl.ds(2 * j + c, 1), :]
-        return pltpu.roll(jnp.broadcast_to(line, (128, 128)), 0, 1, stride=1, stride_axis=0)
-
-    for c in range(2):
-        lanes = slice(c * 128, (c + 1) * 128)
-        first = turned_rows(0, c)
-        toeplitz[0, :, lanes] = jnp.where(after, first, zero).astype(BF16)
-
-        def place(j, before):
-            current = turned_rows(j, c)
-            toeplitz[j, :, lanes] = jnp.where(after, current, before).astype(BF16)
-            return current
-
-        last = lax.fori_loop(1, 32, place, first)
-        toeplitz[32, :, lanes] = jnp.where(after, zero, last).astype(BF16)
+    straight = col < 128 - row
+
+    def place(step):
+        for part in range(3):
+            j = 3 * step + part
+            for c in range(2):
+                block = jnp.broadcast_to(lags[pl.ds(2 * j + 2 + c, 1), :], (128, 128))
+                before = jnp.broadcast_to(lags[pl.ds(2 * j + c, 1), :], (128, 128))
+                tile = pltpu.roll(jnp.where(straight, block, before), 0, 1, stride=1, stride_axis=0)
+                toeplitz[j, :, c * 128:(c + 1) * 128] = tile.astype(BF16)
+
+    each(0, 11, place)
 
     for k in order:
         values_to(k).wait()
 
-    def unpack(l):
-        x = got[l].astype(F32).reshape(16, 128)
-        blocks[32 + l] = x.astype(BF16)
-        blocks[l] = jnp.concatenate([jnp.zeros((2, 128), F32), x[:14]], axis=0).astype(BF16)
-
-    each(0, 32, unpack)
-
-    def left(j):
-        return blocks[pl.ds(32 - j, 32)].reshape(512, 128)
-
-    total[...] = jnp.dot(left(32), toeplitz[32], preferred_element_type=F32)
-
-    def add(k):
-        pair = jnp.concatenate([left(2 * k), left(2 * k + 1)], axis=1)
-        total[...] += jnp.dot(pair, toeplitz[pl.ds(2 * k, 2)].reshape(256, 256), preferred_element_type=F32)
-
-    each(0, 16, add)
-
-    even = lax.rem(lax.broadcasted_iota(jnp.int32, (16, 128), 0), 2) == 0
-
-    def pick(l):
-        both = total[pl.ds(pl.multiple_of(16 * l, 16), 16), :]
-        results[l] = jnp.where(even, both[:, :128], both[:, 128:]).astype(BF16).reshape(8, 2, 128)
-
-    each(0, 32, pick)
+    def unpack(step):
+        for part in range(8):
+            l = 8 * step + part
+            x = got[l].astype(F32).reshape(16, 128)
+            blocks[32 + l] = x.astype(BF16)
+            blocks[l] = jnp.concatenate([jnp.zeros((2, 128), F32), x[:14]], axis=0).astype(BF16)
+
+    each(0, 4, unpack)
+
+    even = lax.rem(lax.broadcasted_iota(jnp.int32, (256, 128), 0), 2) == 0
+
+    for side in range(2):
+        def left(j):
+            return blocks[32 - j + 16 * side:48 - j + 16 * side].reshape(256, 128)
+
+        sums = jnp.dot(left(32), toeplitz[32], preferred_element_type=F32)
+        for k in range(16):
+            pair = jnp.concatenate([left(2 * k), left(2 * k + 1)], axis=1)
+            sums += jnp.dot(pair, toeplitz[2 * k:2 * k + 2].reshape(256, 256), preferred_element_type=F32)
+        chosen = jnp.where(even, sums[:, :128], sums[:, 128:])
+        results[16 * side:16 * side + 16] = chosen.astype(BF16).reshape(16, 8, 2, 128)
     for k in order:
         back_to(k).start()
     back[:, me] = results[pl.ds(16 * odd, 16), high]
@@ -178,8 +167,8 @@
 
 
 def mix_kernel(
-    back_hbm, values_hbm, gates_hbm, skip_ref, weight_hbm, out_ref,
-    back, values, gates, weight, got, hidden, gathered, local_sem, send_sem, recv_sem, side_send, side_recv,
+    back, values_hbm, gates_hbm, skip_ref, weight_hbm, out_ref,
+    values, gates, weight, got, hidden, gathered, local_sem, send_sem, recv_sem, side_send, side_recv,
 ):
     me = lax.axis_index("w")
     my_ch = lax.axis_index("ch")
@@ -188,12 +177,11 @@
     loads = [
         pltpu.make_async_copy(source, target, local_sem.at[k])
         for k, (source, target) in enumerate(
-            ((back_hbm, back), (values_hbm, values), (gates_hbm, gates), (weight_hbm, weight))
+            ((values_hbm, values), (gates_hbm, gates), (weight_hbm, weight))
         )
     ]
     for load in loads:
         load.start()
-    loads[0].wait()
     got[:, me] = back[pl.ds(2 * me, 2)]
     wait_for(NW - 1 + 3)
 
@@ -206,8 +194,8 @@
     order = (4, 3, 5, 2, 6, 1, 7)
     for k in order:
         part_to(k).start()
+    loads[0].wait()
     loads[1].wait()
-    loads[2].wait()
     for k in order:
         part_to(k).wait()
 
@@ -223,7 +211,7 @@
 
     for k in (2, 1, 3):
         side_to(k).start()
-    loads[3].wait()
+    loads[2].wait()
 
     def part(block, channel):
         rows = pl.ds(pl.multiple_of(channel * 256, 256), 256)
@@ -240,7 +228,7 @@
     vmem = pl.BlockSpec(memory_space=VMEM)
     spread = pl.pallas_call(
         spread_kernel,
-        out_shape=jax.ShapeDtypeStruct((18, NZ, 2, 128), BF16),
+        out_shape=pltpu.VMEM((18, NZ, 2, 128), BF16),
         in_specs=[ANY, ANY],
         out_specs=vmem,
         scratch_shapes=[
@@ -251,28 +239,28 @@
     )(values, filter_taps)
     back = pl.pallas_call(
         convolve_kernel,
-        out_shape=jax.ShapeDtypeStruct((16, NZ, 2, 128), BF16),
-        in_specs=[ANY],
+        out_shape=pltpu.VMEM((16, NZ, 2, 128), BF16),
+        in_specs=[vmem],
         out_specs=vmem,
         scratch_shapes=[
-            VMEM((18, NZ, 2, 128), BF16), VMEM((32, 8, 2, 128), BF16), VMEM((NZ, 2, 2, 128), BF16),
-            VMEM((64, 16, 128), BF16), VMEM((64, 128), F32), VMEM((33, 128, 256), BF16), VMEM((512, 256), F32),
-            VMEM((32, 8, 2, 128), BF16), dma, dma((3, NZ)), dma((3, NZ)),
+            VMEM((32, 8, 2, 128), BF16), VMEM((NZ, 2, 2, 128), BF16),
+            VMEM((64, 16, 128), BF16), VMEM((68, 128), F32), VMEM((33, 128, 256), BF16),
+            VMEM((32, 8, 2, 128), BF16), dma((3, NZ)), dma((3, NZ)),
         ],
         compiler_params=pltpu.CompilerParams(collective_id=1, has_side_effects=True),
-    )(spread)
+    )(pltpu.with_memory_space_constraint(spread, VMEM))
     return pl.pallas_call(
         mix_kernel,
         out_shape=jax.ShapeDtypeStruct((256, 512), F32),
-        in_specs=[ANY, ANY, ANY, vmem, ANY],
+        in_specs=[vmem, ANY, ANY, vmem, ANY],
         out_specs=vmem,
         scratch_shapes=[
-            VMEM((16, NZ, 2, 128), BF16), VMEM((256, 256), F32), VMEM((256, 256), F32), VMEM((1024, 512), BF16),
+            VMEM((256, 256), F32), VMEM((256, 256), F32), VMEM((1024, 512), BF16),
             VMEM((2, NW, NZ, 2, 128), BF16), VMEM((256, 256), BF16), VMEM((3, 256, 256), BF16),
-            dma((4,)), dma((NW,)), dma((NW,)), dma((3,)), dma((3,)),
+            dma((3,)), dma((NW,)), dma((NW,)), dma((3,)), dma((3,)),
         ],
         compiler_params=pltpu.CompilerParams(collective_id=2, has_side_effects=True),
-    )(back, values, gates, skip.reshape(1, 256), out_weight)
+    )(pltpu.with_memory_space_constraint(back, VMEM), values, gates, skip.reshape(1, 256), out_weight)
 
 
 def solution(mesh):

time: 71.8 us -> 62.7 us (0.87)
  Pallas kernels: 69.7 us -> 60.6 us
    pallas_call x2, Pallas kernels: 48.1 us -> 39.6 us  [the longest x1 26.1 us: body(): pl.pallas_call(convolve_kernel, out_shape=pltpu.VMEM((16, NZ, 2, 128), BF...]
where the time goes in v2:
time: 62.7 us; the launch traced here: 62.5 us
  Pallas kernels  60.6 us (97%)
  local copies, waits for them, and re-layouts  1.87 us (3%)
    pallas_call x1, Pallas kernels, body(): pl.pallas_call(convolve_kernel, out_shape=pltpu.VMEM((16, NZ, 2, 128), BF...  26.1 us
    pallas_call x1, Pallas kernels, body(): pl.pallas_call(mix_kernel, out_shape=jax.ShapeDtypeStruct((256, 512), F32...  20.9 us
    pallas_call x1, Pallas kernels, body(): pl.pallas_call(spread_kernel, out_shape=pltpu.VMEM((18, NZ, 2, 128), BF16...  13.6 us
    unnamed x1, local copies, waits for them, and re-layouts  1.87 us

profile of v2, /device:TPU:1, one launch (start us, length us, event | category | flops | bytes accessed | tf_op | source)
XLA Modules:
  0.0 62.5 jit_solution(14242110944732584448)
XLA Ops:
  0.0 13.6 %shard_map.55.rows = bf16[18,16,2,128]{3,2,1,0:T(2,128)(2,1)S(1)} custom-call(f32[256,256]{1,0:T(8,128)} %values_hbm.3, f32[32,256]{1,0:T(8,128)} %taps_hbm.1), custom_call_target="tpu_custom_call" | custom-call | tf_op jit(solution)/shard_map/pallas_call | solution.py:229
  13.6 26.1 %shard_map.56.back = bf16[16,16,2,128]{3,2,1,0:T(2,128)(2,1)S(1)} custom-call(bf16[18,16,2,128]{3,2,1,0:T(2,128)(2,1)S(1)} %shard_map.55.rows), custom_call_target="tpu_custom_call" | custom-call | tf_op jit(solution)/shard_map/pallas_call | solution.py:240
  39.6 20.9 %shard_map.57 = f32[256,512]{1,0:T(8,128)} custom-call(bf16[16,16,2,128]{3,2,1,0:T(2,128)(2,1)S(1)} %shard_map.56.back, f32[256,256]{1,0:T(8,128)} %values_hbm.3, f32[256,256]{1,0:T(8,128)} %gates_hbm.1, f32[1,256]{1,0:T(1,128)} %bitcast.1, bf16[1024,512]{1,0:T(8,128)(2,1)} %weight_hbm.1), custom_call_target="tpu_custom_call" | custom-call | tf_op jit(solution)/shard_map/pallas_call | solution.py:252
  60.6 1.9 %copy.7 = f32[256,512]{1,0:T(8,128)} copy(f32[256,512]{1,0:T(8,128)} %shard_map.57) | data formatting | bytes 1048576

commit v3 on v2

--- a/solution.py
+++ b/solution.py
@@ -167,23 +167,24 @@
 
 
 def mix_kernel(
-    back, values_hbm, gates_hbm, skip_ref, weight_hbm, out_ref,
-    values, gates, weight, got, hidden, gathered, local_sem, send_sem, recv_sem, side_send, side_recv,
+    back, values_hbm, gates_hbm, skip_ref, weight_hbm, gathered, weight,
+    values, gates, got, local_sem, send_sem, recv_sem, right_send, left_recv, left_send, right_recv, on_send, on_recv,
 ):
     me = lax.axis_index("w")
     my_ch = lax.axis_index("ch")
+    right, left, across = lax.rem(my_ch + 1, 4), lax.rem(my_ch + 3, 4), lax.rem(my_ch + 2, 4)
     greet("w", NW)
-    greet("ch", 4)
+    barrier = pltpu.get_barrier_semaphore()
+    for peer in (left, right):
+        pl.semaphore_signal(barrier, inc=1, device_id={"ch": peer}, device_id_type=MESH)
     loads = [
         pltpu.make_async_copy(source, target, local_sem.at[k])
-        for k, (source, target) in enumerate(
-            ((values_hbm, values), (gates_hbm, gates), (weight_hbm, weight))
-        )
+        for k, (source, target) in enumerate(((values_hbm, values), (gates_hbm, gates), (weight_hbm, weight)))
     ]
     for load in loads:
         load.start()
     got[:, me] = back[pl.ds(2 * me, 2)]
-    wait_for(NW - 1 + 3)
+    wait_for(NW - 1 + 2)
 
     def part_to(k):
         peer = lax.rem(me + k, NW)
@@ -199,28 +200,68 @@
     for k in order:
         part_to(k).wait()
 
+    def piece(slot, quarter):
+        return gathered.at[slot, pl.ds(64 * quarter, 64)]
+
+    def to_right(quarter):
+        return pltpu.make_async_remote_copy(
+            src_ref=piece(my_ch, quarter), dst_ref=piece(my_ch, quarter), send_sem=right_send.at[quarter],
+            recv_sem=left_recv.at[quarter], device_id={"ch": right}, device_id_type=MESH)
+
+    def to_left(quarter):
+        return pltpu.make_async_remote_copy(
+            src_ref=piece(my_ch, quarter), dst_ref=piece(my_ch, quarter), send_sem=left_send.at[quarter],
+            recv_sem=right_recv.at[quarter], device_id={"ch": left}, device_id_type=MESH)
+
+    def pass_on(quarter):
+        source, target = (left, right) if quarter < 2 else (right, left)
+        return pltpu.make_async_remote_copy(
+            src_ref=piece(source, quarter), dst_ref=piece(source, quarter), send_sem=on_send.at[quarter],
+            recv_sem=on_recv.at[quarter], device_id={"ch": target}, device_id_type=MESH)
+
     for half in range(2):
         rows = slice(half * 128, (half + 1) * 128)
         convolved = got[half].astype(F32).reshape(256, 128).T
-        hidden[rows, :] = (gates[rows, :] * (convolved + skip_ref[...] * values[rows, :])).astype(BF16)
-
-    def side_to(k):
-        return pltpu.make_async_remote_copy(
-            src_ref=hidden, dst_ref=gathered.at[k - 1], send_sem=side_send.at[k - 1],
-            recv_sem=side_recv.at[k - 1], device_id={"ch": lax.rem(my_ch + k, 4)}, device_id_type=MESH)
-
-    for k in (2, 1, 3):
-        side_to(k).start()
+        hidden = (gates[rows, :] * (convolved + skip_ref[...] * values[rows, :])).astype(BF16)
+        gathered[my_ch, rows, :] = hidden
+        for quarter in (2 * half, 2 * half + 1):
+            (to_left if half else to_right)(quarter).start()
+    for quarter in (2, 3):
+        to_right(quarter).start()
+    for quarter in (0, 1):
+        to_left(quarter).start()
+    for first, second in ((0, 2), (1, 3)):
+        to_right(first).wait_recv()
+        pass_on(first).start()
+        to_left(second).wait_recv()
+        pass_on(second).start()
     loads[2].wait()
-
-    def part(block, channel):
-        rows = pl.ds(pl.multiple_of(channel * 256, 256), 256)
-        return jnp.dot(block, weight[rows, :], preferred_element_type=F32)
-
-    out_ref[...] = part(hidden[...], my_ch)
-    for k in (1, 3, 2):
-        side_to(k).wait()
-        out_ref[...] += part(gathered[k - 1], lax.rem(my_ch + 4 - k, 4))
+    for quarter in (2, 3):
+        to_right(quarter).wait_recv()
+    for quarter in (0, 1):
+        to_left(quarter).wait_recv()
+    for quarter in range(4):
+        to_right(quarter).wait_send()
+        to_left(quarter).wait_send()
+        pass_on(quarter).wait()
+
+
+def output_kernel(gathered, weight, out_hbm, out, out_sem):
+    def store(half):
+        rows = pl.ds(128 * half, 128)
+        return pltpu.make_async_copy(out.at[rows], out_hbm.at[rows], out_sem.at[half])
+
+    for half in range(2):
+        rows = slice(128 * half, 128 * half + 128)
+        for side in range(2):
+            lanes = slice(256 * side, 256 * side + 256)
+            sums = jnp.dot(gathered[0, rows, :], weight[0:256, lanes], preferred_element_type=F32)
+            for k in range(1, 4):
+                sums += jnp.dot(gathered[k, rows, :], weight[256 * k:256 * k + 256, lanes], preferred_element_type=F32)
+            out[rows, lanes] = sums
+        store(half).start()
+    for half in range(2):
+        store(half).wait()
 
 
 def body(values, gates, filter_taps, skip, out_weight):
@@ -249,18 +290,25 @@
         ],
         compiler_params=pltpu.CompilerParams(collective_id=1, has_side_effects=True),
     )(pltpu.with_memory_space_constraint(spread, VMEM))
-    return pl.pallas_call(
+    near = lambda x: pltpu.with_memory_space_constraint(x, VMEM)
+    gathered, weight = pl.pallas_call(
         mix_kernel,
-        out_shape=jax.ShapeDtypeStruct((256, 512), F32),
+        out_shape=(VMEM((4, 256, 256), BF16), VMEM((1024, 512), BF16)),
         in_specs=[vmem, ANY, ANY, vmem, ANY],
-        out_specs=vmem,
+        out_specs=(vmem, vmem),
         scratch_shapes=[
-            VMEM((256, 256), F32), VMEM((256, 256), F32), VMEM((1024, 512), BF16),
-            VMEM((2, NW, NZ, 2, 128), BF16), VMEM((256, 256), BF16), VMEM((3, 256, 256), BF16),
-            dma((3,)), dma((NW,)), dma((NW,)), dma((3,)), dma((3,)),
+            VMEM((256, 256), F32), VMEM((256, 256), F32), VMEM((2, NW, NZ, 2, 128), BF16),
+            dma((3,)), dma((NW,)), dma((NW,)), dma((4,)), dma((4,)), dma((4,)), dma((4,)), dma((4,)), dma((4,)),
         ],
         compiler_params=pltpu.CompilerParams(collective_id=2, has_side_effects=True),
-    )(pltpu.with_memory_space_constraint(back, VMEM), values, gates, skip.reshape(1, 256), out_weight)
+    )(near(back), values, gates, skip.reshape(1, 256), out_weight)
+    return pl.pallas_call(
+        output_kernel,
+        out_shape=jax.ShapeDtypeStruct((256, 512), F32),
+        in_specs=[vmem, vmem],
+        out_specs=ANY,
+        scratch_shapes=[VMEM((256, 512), F32), dma((2,))],
+    )(near(gathered), near(weight))
 
 
 def solution(mesh):

time: 62.7 us -> 58.9 us (0.939)
  Pallas kernels: 60.6 us -> 58.5 us
  local copies, waits for them, and re-layouts: 1.87 us -> 0 us
    pallas_call x1 -> x2, Pallas kernels: 20.9 us -> 18.9 us  [the longest x1 17.7 us: body(): pl.pallas_call(mix_kernel, out_shape=(VMEM((4, 256, 256), BF16), VMEM((10...]
    unnamed x1 -> x0, local copies, waits for them, and re-layouts: 1.87 us -> none
where the time goes in v3:
time: 58.9 us; the launch traced here: 58.5 us
  Pallas kernels  58.5 us (99%)
    pallas_call x1, Pallas kernels, body(): pl.pallas_call(convolve_kernel, out_shape=pltpu.VMEM((16, NZ, 2, 128), BF...  26.1 us
    pallas_call x1, Pallas kernels, body(): pl.pallas_call(mix_kernel, out_shape=(VMEM((4, 256, 256), BF16), VMEM((10...  17.7 us
    pallas_call x1, Pallas kernels, body(): pl.pallas_call(spread_kernel, out_shape=pltpu.VMEM((18, NZ, 2, 128), BF16...  13.6 us

profile of v3, /device:TPU:1, one launch (start us, length us, event | category | flops | bytes accessed | tf_op | source)
XLA Modules:
  0.0 58.5 jit_solution(17884427886127119387)
XLA Ops:
  0.0 13.6 %shard_map.55.rows = bf16[18,16,2,128]{3,2,1,0:T(2,128)(2,1)S(1)} custom-call(f32[256,256]{1,0:T(8,128)} %values_hbm.3, f32[32,256]{1,0:T(8,128)} %taps_hbm.1), custom_call_target="tpu_custom_call" | custom-call | tf_op jit(solution)/shard_map/pallas_call | solution.py:270
  13.6 26.1 %shard_map.56.back = bf16[16,16,2,128]{3,2,1,0:T(2,128)(2,1)S(1)} custom-call(bf16[18,16,2,128]{3,2,1,0:T(2,128)(2,1)S(1)} %shard_map.55.rows), custom_call_target="tpu_custom_call" | custom-call | tf_op jit(solution)/shard_map/pallas_call | solution.py:281
  39.6 17.7 %shard_map.57 = (bf16[4,256,256]{2,1,0:T(8,128)(2,1)S(1)}, bf16[1024,512]{1,0:T(8,128)(2,1)S(1)}) custom-call(bf16[16,16,2,128]{3,2,1,0:T(2,128)(2,1)S(1)} %shard_map.56.back, f32[256,256]{1,0:T(8,128)} %values_hbm.3, f32[256,256]{1,0:T(8,128)} %gates_hbm.1, f32[1,256]{1,0:T(1,128)} %bitcast.1, bf16[1024,512]{1,0:T(8,128)(2,1)} %weight_hbm.1), custom_call_target="tpu_custom_call" | custom-call | tf_op jit(solution)/shard_map/pallas_call | solution.py:294
  57.4 1.2 %shard_map.58 = f32[256,512]{1,0:T(8,128)} custom-call(bf16[4,256,256]{2,1,0:T(8,128)(2,1)S(1)} %get-tuple-element.7.gathered, bf16[1024,512]{1,0:T(8,128)(2,1)S(1)} %get-tuple-element.8.weight), custom_call_target="tpu_custom_call" | custom-call | tf_op jit(solution)/shard_map/pallas_call | solution.py:305

commit v4 on v3

--- a/solution.py
+++ b/solution.py
@@ -46,12 +46,16 @@
         load.start()
     loads[0].wait()
     own = jnp.concatenate([taps[...], jnp.zeros((96, 256), F32)], axis=0)
-    own = pltpu.roll(own.T, 32 * lax.rem(me, 4), 1)
-    send_taps[...] = own.astype(BF16).reshape(NW, NZ, 2, 128)
+    turned = own.T
+    packed = turned[0:64] + pltpu.roll(turned[64:128], 32, 1)
+    packed += pltpu.roll(turned[128:192], 64, 1) + pltpu.roll(turned[192:256], 96, 1)
+    send_taps[...] = packed.astype(BF16).reshape(NW, 8, 128)
     loads[1].wait()
     for half in range(2):
         turned = values[half * 128:(half + 1) * 128, :].T
-        send_values[half] = turned.astype(BF16).reshape(NW, NZ, 2, 128)
+        for w in range(NW):
+            own = jnp.concatenate([turned[64 * q + 8 * w:64 * q + 8 * w + 8] for q in range(4)], axis=0)
+            send_values[half, w] = own.astype(BF16).reshape(NZ, 2, 128)
     wait_for(NW - 1)
 
     def taps_to(k):
@@ -74,10 +78,17 @@
     got_taps[0] = send_taps[me]
     for k in order:
         taps_to(k).wait()
-    for half in range(2):
-        from_w = lambda w: got_taps[lax.rem(me + NW - w, NW)]
-        w = 4 * half
-        out[16 + half] = (from_w(w) + from_w(w + 1)) + (from_w(w + 2) + from_w(w + 3))
+    lane = lax.broadcasted_iota(jnp.int32, (8, 128), 1)
+    for half in range(2):
+        parts = [got_taps[lax.rem(me + NW - w, NW)].astype(F32) for w in range(4 * half, 4 * half + 4)]
+        rows = []
+        for q in range(4):
+            line = pltpu.roll(parts[3], 32 * ((3 - q) % 4), 1) if q != 3 else parts[3]
+            for k in range(3):
+                moved = pltpu.roll(parts[k], 32 * ((k - q) % 4), 1) if k != q else parts[k]
+                line = jnp.where((lane >= 32 * k) & (lane < 32 * k + 32), moved, line)
+            rows.append(line)
+        out[16 + half] = jnp.concatenate(rows, axis=0).astype(BF16).reshape(NZ, 2, 128)
     for k in order:
         values_to(k).wait()
 
@@ -221,7 +232,9 @@
 
     for half in range(2):
         rows = slice(half * 128, (half + 1) * 128)
-        convolved = got[half].astype(F32).reshape(256, 128).T
+        arrived = got[half].astype(F32).reshape(256, 128)
+        convolved = jnp.concatenate(
+            [arrived[32 * w + 8 * q:32 * w + 8 * q + 8] for q in range(4) for w in range(NW)], axis=0).T
         hidden = (gates[rows, :] * (convolved + skip_ref[...] * values[rows, :])).astype(BF16)
         gathered[my_ch, rows, :] = hidden
         for quarter in (2 * half, 2 * half + 1):
@@ -274,7 +287,7 @@
         out_specs=vmem,
         scratch_shapes=[
             VMEM((256, 256), F32), VMEM((32, 256), F32), VMEM((2, NW, NZ, 2, 128), BF16),
-            VMEM((NW, NZ, 2, 128), BF16), VMEM((NW, NZ, 2, 128), BF16), dma((2,)), dma((2, NW)), dma((2, NW)),
+            VMEM((NW, 8, 128), BF16), VMEM((NW, 8, 128), BF16), dma((2,)), dma((2, NW)), dma((2, NW)),
         ],
         compiler_params=pltpu.CompilerParams(collective_id=0, has_side_effects=True),
     )(values, filter_taps)

time: 58.9 us -> 58.7 us (level)
  no operation moved by 1% of the time
where the time goes in v4:
time: 58.7 us; the launch traced here: 58.5 us
  Pallas kernels  58.5 us (100%)
    pallas_call x1, Pallas kernels, body(): pl.pallas_call(convolve_kernel, out_shape=pltpu.VMEM((16, NZ, 2, 128), BF...  26.1 us
    pallas_call x1, Pallas kernels, body(): pl.pallas_call(mix_kernel, out_shape=(VMEM((4, 256, 256), BF16), VMEM((10...  18.2 us
    pallas_call x1, Pallas kernels, body(): pl.pallas_call(spread_kernel, out_shape=pltpu.VMEM((18, NZ, 2, 128), BF16...  13.1 us

profile of v4, /device:TPU:1, one launch (start us, length us, event | category | flops | bytes accessed | tf_op | source)
XLA Modules:
  0.0 58.5 jit_solution(184944196957547475)
XLA Ops:
  0.0 13.1 %shard_map.55.rows = bf16[18,16,2,128]{3,2,1,0:T(2,128)(2,1)S(1)} custom-call(f32[256,256]{1,0:T(8,128)} %values_hbm.3, f32[32,256]{1,0:T(8,128)} %taps_hbm.1), custom_call_target="tpu_custom_call" | custom-call | tf_op jit(solution)/shard_map/pallas_call | solution.py:283
  13.1 26.1 %shard_map.56.back = bf16[16,16,2,128]{3,2,1,0:T(2,128)(2,1)S(1)} custom-call(bf16[18,16,2,128]{3,2,1,0:T(2,128)(2,1)S(1)} %shard_map.55.rows), custom_call_target="tpu_custom_call" | custom-call | tf_op jit(solution)/shard_map/pallas_call | solution.py:294
  39.2 18.2 %shard_map.57 = (bf16[4,256,256]{2,1,0:T(8,128)(2,1)S(1)}, bf16[1024,512]{1,0:T(8,128)(2,1)S(1)}) custom-call(bf16[16,16,2,128]{3,2,1,0:T(2,128)(2,1)S(1)} %shard_map.56.back, f32[256,256]{1,0:T(8,128)} %values_hbm.3, f32[256,256]{1,0:T(8,128)} %gates_hbm.1, f32[1,256]{1,0:T(1,128)} %bitcast.1, bf16[1024,512]{1,0:T(8,128)(2,1)} %weight_hbm.1), custom_call_target="tpu_custom_call" | custom-call | tf_op jit(solution)/shard_map/pallas_call | solution.py:307
  57.3 1.2 %shard_map.58 = f32[256,512]{1,0:T(8,128)} custom-call(bf16[4,256,256]{2,1,0:T(8,128)(2,1)S(1)} %get-tuple-element.7.gathered, bf16[1024,512]{1,0:T(8,128)(2,1)S(1)} %get-tuple-element.8.weight), custom_call_target="tpu_custom_call" | custom-call | tf_op jit(solution)/shard_map/pallas_call | solution.py:318

commit v5 on v4

--- a/solution.py
+++ b/solution.py
@@ -35,8 +35,13 @@
     pl.semaphore_wait(pltpu.get_barrier_semaphore(), count)
 
 
-def spread_kernel(values_hbm, taps_hbm, out, values, taps, send_values, send_taps, got_taps, local_sem, send_sem, recv_sem):
-    me = lax.axis_index("w")
+def convolve_kernel(
+    values_hbm, taps_hbm, back, values, taps, send_values, send_taps, near_taps, rows, got, got_taps, blocks, lags,
+    toeplitz, results, local_sem, near_send, near_recv, send_sem, recv_sem,
+):
+    at = lax.axis_index("w")
+    me = lax.axis_index("z")
+    greet("z", NZ)
     greet("w", NW)
     loads = [
         pltpu.make_async_copy(taps_hbm, taps, local_sem.at[0]),
@@ -56,50 +61,45 @@
         for w in range(NW):
             own = jnp.concatenate([turned[64 * q + 8 * w:64 * q + 8 * w + 8] for q in range(4)], axis=0)
             send_values[half, w] = own.astype(BF16).reshape(NZ, 2, 128)
-    wait_for(NW - 1)
-
-    def taps_to(k):
-        peer = lax.rem(me + k, NW)
-        return pltpu.make_async_remote_copy(
-            src_ref=send_taps.at[peer], dst_ref=got_taps.at[k], send_sem=send_sem.at[0, k],
-            recv_sem=recv_sem.at[0, k], device_id={"w": peer}, device_id_type=MESH)
-
-    def values_to(k):
-        peer = lax.rem(me + k, NW)
-        return pltpu.make_async_remote_copy(
-            src_ref=send_values.at[:, peer], dst_ref=out.at[pl.ds(2 * me, 2)], send_sem=send_sem.at[1, k],
-            recv_sem=recv_sem.at[1, k], device_id={"w": peer}, device_id_type=MESH)
-
-    order = (4, 3, 5, 2, 6, 1, 7)
-    for k in order:
-        taps_to(k).start()
-        values_to(k).start()
-    out[pl.ds(2 * me, 2)] = send_values[:, me]
-    got_taps[0] = send_taps[me]
-    for k in order:
-        taps_to(k).wait()
+    wait_for(NW - 1 + NZ - 1)
+
+    def taps_near(k):
+        peer = lax.rem(at + k, NW)
+        return pltpu.make_async_remote_copy(
+            src_ref=send_taps.at[peer], dst_ref=near_taps.at[k], send_sem=near_send.at[0, k],
+            recv_sem=near_recv.at[0, k], device_id={"w": peer}, device_id_type=MESH)
+
+    def values_near(k):
+        peer = lax.rem(at + k, NW)
+        return pltpu.make_async_remote_copy(
+            src_ref=send_values.at[:, peer], dst_ref=rows.at[pl.ds(2 * at, 2)], send_sem=near_send.at[1, k],
+            recv_sem=near_recv.at[1, k], device_id={"w": peer}, device_id_type=MESH)
+
+    near_order = (4, 3, 5, 2, 6, 1, 7)
+    for k in near_order:
+        taps_near(k).start()
+        values_near(k).start()
+    rows[pl.ds(2 * at, 2)] = send_values[:, at]
+    near_taps[0] = send_taps[at]
+    for k in near_order:
+        taps_near(k).wait()
     lane = lax.broadcasted_iota(jnp.int32, (8, 128), 1)
     for half in range(2):
-        parts = [got_taps[lax.rem(me + NW - w, NW)].astype(F32) for w in range(4 * half, 4 * half + 4)]
-        rows = []
+        parts = [near_taps[lax.rem(at + NW - w, NW)].astype(F32) for w in range(4 * half, 4 * half + 4)]
+        lines = []
         for q in range(4):
             line = pltpu.roll(parts[3], 32 * ((3 - q) % 4), 1) if q != 3 else parts[3]
             for k in range(3):
                 moved = pltpu.roll(parts[k], 32 * ((k - q) % 4), 1) if k != q else parts[k]
                 line = jnp.where((lane >= 32 * k) & (lane < 32 * k + 32), moved, line)
-            rows.append(line)
-        out[16 + half] = jnp.concatenate(rows, axis=0).astype(BF16).reshape(NZ, 2, 128)
-    for k in order:
-        values_to(k).wait()
-
-
-def convolve_kernel(rows, back, got, got_taps, blocks, lags, toeplitz, results, send_sem, recv_sem):
-    me = lax.axis_index("z")
-    greet("z", NZ)
+            lines.append(line)
+        rows[16 + half] = jnp.concatenate(lines, axis=0).astype(BF16).reshape(NZ, 2, 128)
+    for k in near_order:
+        values_near(k).wait()
+
     odd, high = lax.rem(me, 2), me // 2
     got[pl.ds(16 * odd, 16), high] = rows[0:16, me]
     got_taps[me] = rows[16:18, me]
-    wait_for(NZ - 1)
 
     def taps_to(k):
         peer = lax.rem(me + k, NZ)
@@ -280,29 +280,20 @@
 def body(values, gates, filter_taps, skip, out_weight):
     dma = pltpu.SemaphoreType.DMA
     vmem = pl.BlockSpec(memory_space=VMEM)
-    spread = pl.pallas_call(
-        spread_kernel,
-        out_shape=pltpu.VMEM((18, NZ, 2, 128), BF16),
+    back = pl.pallas_call(
+        convolve_kernel,
+        out_shape=VMEM((16, NZ, 2, 128), BF16),
         in_specs=[ANY, ANY],
         out_specs=vmem,
         scratch_shapes=[
             VMEM((256, 256), F32), VMEM((32, 256), F32), VMEM((2, NW, NZ, 2, 128), BF16),
-            VMEM((NW, 8, 128), BF16), VMEM((NW, 8, 128), BF16), dma((2,)), dma((2, NW)), dma((2, NW)),
-        ],
-        compiler_params=pltpu.CompilerParams(collective_id=0, has_side_effects=True),
-    )(values, filter_taps)
-    back = pl.pallas_call(
-        convolve_kernel,
-        out_shape=pltpu.VMEM((16, NZ, 2, 128), BF16),
-        in_specs=[vmem],
-        out_specs=vmem,
-        scratch_shapes=[
-            VMEM((32, 8, 2, 128), BF16), VMEM((NZ, 2, 2, 128), BF16),
-            VMEM((64, 16, 128), BF16), VMEM((68, 128), F32), VMEM((33, 128, 256), BF16),
-            VMEM((32, 8, 2, 128), BF16), dma((3, NZ)), dma((3, NZ)),
+            VMEM((NW, 8, 128), BF16), VMEM((NW, 8, 128), BF16), VMEM((18, NZ, 2, 128), BF16),
+            VMEM((32, 8, 2, 128), BF16), VMEM((NZ, 2, 2, 128), BF16), VMEM((64, 16, 128), BF16),
+            VMEM((68, 128), F32), VMEM((33, 128, 256), BF16), VMEM((32, 8, 2, 128), BF16),
+            dma((2,)), dma((2, NW)), dma((2, NW)), dma((3, NZ)), dma((3, NZ)),
         ],
         compiler_params=pltpu.CompilerParams(collective_id=1, has_side_effects=True),
-    )(pltpu.with_memory_space_constraint(spread, VMEM))
+    )(values, filter_taps)
     near = lambda x: pltpu.with_memory_space_constraint(x, VMEM)
     gathered, weight = pl.pallas_call(
         mix_kernel,

time: 58.7 us -> 56.7 us (0.966)
  Pallas kernels: 58.5 us -> 56.6 us
    pallas_call x1, Pallas kernels: 18.2 us -> 16.6 us  [body(): pl.pallas_call(mix_kernel, out_shape=(VMEM((4, 256, 256), BF16), VMEM((10...]
    pallas_call x2 -> x1, Pallas kernels: 39.2 us -> 38.8 us  [body(): pl.pallas_call(convolve_kernel, out_shape=VMEM((16, NZ, 2, 128), BF16), i...]
where the time goes in v5:
time: 56.7 us; the launch traced here: 56.6 us
  Pallas kernels  56.6 us (100%)
    pallas_call x1, Pallas kernels, body(): pl.pallas_call(convolve_kernel, out_shape=VMEM((16, NZ, 2, 128), BF16), i...  38.8 us
    pallas_call x1, Pallas kernels, body(): pl.pallas_call(mix_kernel, out_shape=(VMEM((4, 256, 256), BF16), VMEM((10...  16.6 us
    pallas_call x1, Pallas kernels, body(): pl.pallas_call(output_kernel, out_shape=jax.ShapeDtypeStruct((256, 512),...  1.16 us

profile of v5, /device:TPU:1, one launch (start us, length us, event | category | flops | bytes accessed | tf_op | source)
XLA Modules:
  0.0 56.6 jit_solution(4097809451919309967)
XLA Ops:
  0.0 38.8 %shard_map.55.back = bf16[16,16,2,128]{3,2,1,0:T(2,128)(2,1)S(1)} custom-call(f32[256,256]{1,0:T(8,128)} %values_hbm.3, f32[32,256]{1,0:T(8,128)} %taps_hbm.1), custom_call_target="tpu_custom_call" | custom-call | tf_op jit(solution)/shard_map/pallas_call | solution.py:283
  38.8 16.6 %shard_map.56 = (bf16[4,256,256]{2,1,0:T(8,128)(2,1)S(1)}, bf16[1024,512]{1,0:T(8,128)(2,1)S(1)}) custom-call(bf16[16,16,2,128]{3,2,1,0:T(2,128)(2,1)S(1)} %shard_map.55.back, f32[256,256]{1,0:T(8,128)} %values_hbm.3, f32[256,256]{1,0:T(8,128)} %gates_hbm.1, f32[1,256]{1,0:T(1,128)} %bitcast.1, bf16[1024,512]{1,0:T(8,128)(2,1)} %weight_hbm.1), custom_call_target="tpu_custom_call" | custom-call | tf_op jit(solution)/shard_map/pallas_call | solution.py:298
  55.4 1.2 %shard_map.57 = f32[256,512]{1,0:T(8,128)} custom-call(bf16[4,256,256]{2,1,0:T(8,128)(2,1)S(1)} %get-tuple-element.7.gathered, bf16[1024,512]{1,0:T(8,128)(2,1)S(1)} %get-tuple-element.8.weight), custom_call_target="tpu_custom_call" | custom-call | tf_op jit(solution)/shard_map/pallas_call | solution.py:309

commit v6 on v5

--- a/solution.py
+++ b/solution.py
@@ -37,7 +37,7 @@
 
 def convolve_kernel(
     values_hbm, taps_hbm, back, values, taps, send_values, send_taps, near_taps, rows, got, got_taps, blocks, lags,
-    toeplitz, results, local_sem, near_send, near_recv, send_sem, recv_sem,
+    toeplitz, results, local_sem, near_send, near_recv, send_sem, recv_sem, back_send, back_recv,
 ):
     at = lax.axis_index("w")
     me = lax.axis_index("z")
@@ -114,10 +114,11 @@
             recv_sem=recv_sem.at[1, k], device_id={"z": peer}, device_id_type=MESH)
 
     def back_to(k):
-        peer = lax.rem(me + k, NZ)
-        return pltpu.make_async_remote_copy(
-            src_ref=results.at[pl.ds(16 * lax.rem(peer, 2), 16), peer // 2], dst_ref=back.at[:, me],
-            send_sem=send_sem.at[2, k], recv_sem=recv_sem.at[2, k], device_id={"z": peer}, device_id_type=MESH)
+        peer = lax.rem(NW * me + at + k, NW * NZ)
+        z, w = peer // NW, lax.rem(peer, NW)
+        return pltpu.make_async_remote_copy(
+            src_ref=results.at[pl.ds(16 * lax.rem(z, 2) + 2 * w, 2), z // 2], dst_ref=back.at[:, at, me],
+            send_sem=back_send.at[k], recv_sem=back_recv.at[k], device_id={"z": z, "w": w}, device_id_type=MESH)
 
     order = (8, 7, 9, 6, 10, 5, 11, 4, 12, 3, 13, 2, 14, 1, 15)
     for k in order:
@@ -170,21 +171,23 @@
             sums += jnp.dot(pair, toeplitz[2 * k:2 * k + 2].reshape(256, 256), preferred_element_type=F32)
         chosen = jnp.where(even, sums[:, :128], sums[:, 128:])
         results[16 * side:16 * side + 16] = chosen.astype(BF16).reshape(16, 8, 2, 128)
-    for k in order:
-        back_to(k).start()
-    back[:, me] = results[pl.ds(16 * odd, 16), high]
-    for k in order:
-        back_to(k).wait()
+    back_to(64).start()
+
+    def far_first(k):
+        back_to(64 + k).start()
+        back_to(64 - k).start()
+
+    each(1, 64, far_first)
+    back[:, at, me] = results[pl.ds(16 * odd + 2 * at, 2), high]
+    each(1, 128, lambda k: back_to(k).wait())
 
 
 def mix_kernel(
     back, values_hbm, gates_hbm, skip_ref, weight_hbm, gathered, weight,
-    values, gates, got, local_sem, send_sem, recv_sem, right_send, left_recv, left_send, right_recv, on_send, on_recv,
+    values, gates, local_sem, right_send, left_recv, left_send, right_recv, on_send, on_recv,
 ):
-    me = lax.axis_index("w")
     my_ch = lax.axis_index("ch")
     right, left, across = lax.rem(my_ch + 1, 4), lax.rem(my_ch + 3, 4), lax.rem(my_ch + 2, 4)
-    greet("w", NW)
     barrier = pltpu.get_barrier_semaphore()
     for peer in (left, right):
         pl.semaphore_signal(barrier, inc=1, device_id={"ch": peer}, device_id_type=MESH)
@@ -194,22 +197,9 @@
     ]
     for load in loads:
         load.start()
-    got[:, me] = back[pl.ds(2 * me, 2)]
-    wait_for(NW - 1 + 2)
-
-    def part_to(k):
-        peer = lax.rem(me + k, NW)
-        return pltpu.make_async_remote_copy(
-            src_ref=back.at[pl.ds(2 * peer, 2)], dst_ref=got.at[:, me], send_sem=send_sem.at[k],
-            recv_sem=recv_sem.at[k], device_id={"w": peer}, device_id_type=MESH)
-
-    order = (4, 3, 5, 2, 6, 1, 7)
-    for k in order:
-        part_to(k).start()
     loads[0].wait()
     loads[1].wait()
-    for k in order:
-        part_to(k).wait()
+    wait_for(2)
 
     def piece(slot, quarter):
         return gathered.at[slot, pl.ds(64 * quarter, 64)]
@@ -232,7 +222,7 @@
 
     for half in range(2):
         rows = slice(half * 128, (half + 1) * 128)
-        arrived = got[half].astype(F32).reshape(256, 128)
+        arrived = back[half].astype(F32).reshape(256, 128)
         convolved = jnp.concatenate(
             [arrived[32 * w + 8 * q:32 * w + 8 * q + 8] for q in range(4) for w in range(NW)], axis=0).T
         hidden = (gates[rows, :] * (convolved + skip_ref[...] * values[rows, :])).astype(BF16)
@@ -282,7 +272,7 @@
     vmem = pl.BlockSpec(memory_space=VMEM)
     back = pl.pallas_call(
         convolve_kernel,
-        out_shape=VMEM((16, NZ, 2, 128), BF16),
+        out_shape=VMEM((2, NW, NZ, 2, 128), BF16),
         in_specs=[ANY, ANY],
         out_specs=vmem,
         scratch_shapes=[
@@ -290,7 +280,7 @@
             VMEM((NW, 8, 128), BF16), VMEM((NW, 8, 128), BF16), VMEM((18, NZ, 2, 128), BF16),
             VMEM((32, 8, 2, 128), BF16), VMEM((NZ, 2, 2, 128), BF16), VMEM((64, 16, 128), BF16),
             VMEM((68, 128), F32), VMEM((33, 128, 256), BF16), VMEM((32, 8, 2, 128), BF16),
-            dma((2,)), dma((2, NW)), dma((2, NW)), dma((3, NZ)), dma((3, NZ)),
+            dma((2,)), dma((2, NW)), dma((2, NW)), dma((2, NZ)), dma((2, NZ)), dma((128,)), dma((128,)),
         ],
         compiler_params=pltpu.CompilerParams(collective_id=1, has_side_effects=True),
     )(values, filter_taps)
@@ -301,8 +291,8 @@
         in_specs=[vmem, ANY, ANY, vmem, ANY],
         out_specs=(vmem, vmem),
         scratch_shapes=[
-            VMEM((256, 256), F32), VMEM((256, 256), F32), VMEM((2, NW, NZ, 2, 128), BF16),
-            dma((3,)), dma((NW,)), dma((NW,)), dma((4,)), dma((4,)), dma((4,)), dma((4,)), dma((4,)), dma((4,)),
+            VMEM((256, 256), F32), VMEM((256, 256), F32),
+            dma((3,)), dma((4,)), dma((4,)), dma((4,)), dma((4,)), dma((4,)), dma((4,)),
         ],
         compiler_params=pltpu.CompilerParams(collective_id=2, has_side_effects=True),
     )(near(back), values, gates, skip.reshape(1, 256), out_weight)

time: 56.7 us -> 55.7 us (0.982)
  Pallas kernels: 56.6 us -> 55.2 us
    pallas_call x1, Pallas kernels: 16.6 us -> 10 us  [body(): pl.pallas_call(mix_kernel, out_shape=(VMEM((4, 256, 256), BF16), VMEM((10...]
    pallas_call x1, Pallas kernels: 38.8 us -> 44.1 us  [body(): pl.pallas_call(convolve_kernel, out_shape=VMEM((2, NW, NZ, 2, 128), BF16)...]
where the time goes in v6:
time: 55.7 us; the launch traced here: 55.2 us
  Pallas kernels  55.2 us (99%)
    pallas_call x1, Pallas kernels, body(): pl.pallas_call(convolve_kernel, out_shape=VMEM((2, NW, NZ, 2, 128), BF16)...  44.1 us
    pallas_call x1, Pallas kernels, body(): pl.pallas_call(mix_kernel, out_shape=(VMEM((4, 256, 256), BF16), VMEM((10...  10 us
    pallas_call x1, Pallas kernels, body(): pl.pallas_call(output_kernel, out_shape=jax.ShapeDtypeStruct((256, 512),...  1.16 us

profile of v6, /device:TPU:1, one launch (start us, length us, event | category | flops | bytes accessed | tf_op | source)
XLA Modules:
  0.0 55.2 jit_solution(740553173609761231)
XLA Ops:
  0.0 44.1 %shard_map.55.back = bf16[2,8,16,2,128]{4,3,2,1,0:T(2,128)(2,1)S(1)} custom-call(f32[256,256]{1,0:T(8,128)} %values_hbm.3, f32[32,256]{1,0:T(8,128)} %taps_hbm.1), custom_call_target="tpu_custom_call" | custom-call | tf_op jit(solution)/shard_map/pallas_call | solution.py:273
  44.1 10.0 %shard_map.56 = (bf16[4,256,256]{2,1,0:T(8,128)(2,1)S(1)}, bf16[1024,512]{1,0:T(8,128)(2,1)S(1)}) custom-call(bf16[2,8,16,2,128]{4,3,2,1,0:T(2,128)(2,1)S(1)} %shard_map.55.back, f32[256,256]{1,0:T(8,128)} %values_hbm.3, f32[256,256]{1,0:T(8,128)} %gates_hbm.1, f32[1,256]{1,0:T(1,128)} %bitcast.1, bf16[1024,512]{1,0:T(8,128)(2,1)} %weight_hbm.1), custom_call_target="tpu_custom_call" | custom-call | tf_op jit(solution)/shard_map/pallas_call | solution.py:288
  54.1 1.2 %shard_map.57 = f32[256,512]{1,0:T(8,128)} custom-call(bf16[4,256,256]{2,1,0:T(8,128)(2,1)S(1)} %get-tuple-element.7.gathered, bf16[1024,512]{1,0:T(8,128)(2,1)S(1)} %get-tuple-element.8.weight), custom_call_target="tpu_custom_call" | custom-call | tf_op jit(solution)/shard_map/pallas_call | solution.py:299

commit v7 on v6

--- a/solution.py
+++ b/solution.py
@@ -94,11 +94,8 @@
                 line = jnp.where((lane >= 32 * k) & (lane < 32 * k + 32), moved, line)
             lines.append(line)
         rows[16 + half] = jnp.concatenate(lines, axis=0).astype(BF16).reshape(NZ, 2, 128)
-    for k in near_order:
-        values_near(k).wait()
 
     odd, high = lax.rem(me, 2), me // 2
-    got[pl.ds(16 * odd, 16), high] = rows[0:16, me]
     got_taps[me] = rows[16:18, me]
 
     def taps_to(k):
@@ -123,6 +120,9 @@
     order = (8, 7, 9, 6, 10, 5, 11, 4, 12, 3, 13, 2, 14, 1, 15)
     for k in order:
         taps_to(k).start()
+    for k in near_order:
+        values_near(k).wait()
+    got[pl.ds(16 * odd, 16), high] = rows[0:16, me]
     for k in order:
         values_to(k).start()
     for k in order:
@@ -173,13 +173,21 @@
         results[16 * side:16 * side + 16] = chosen.astype(BF16).reshape(16, 8, 2, 128)
     back_to(64).start()
 
-    def far_first(k):
-        back_to(64 + k).start()
-        back_to(64 - k).start()
-
-    each(1, 64, far_first)
+    def far_first(step):
+        for k in range(1, 4):
+            back_to(64 + 3 * step + k).start()
+            back_to(64 - 3 * step - k).start()
+
+    each(0, 21, far_first)
     back[:, at, me] = results[pl.ds(16 * odd + 2 * at, 2), high]
-    each(1, 128, lambda k: back_to(k).wait())
+
+    def near_first(step):
+        for k in range(1, 4):
+            back_to(3 * step + k).wait()
+            back_to(128 - 3 * step - k).wait()
+
+    each(0, 21, near_first)
+    back_to(64).wait()
 
 
 def mix_kernel(

time: 55.7 us -> 55.4 us (level)
  Pallas kernels: 55.2 us -> 54.6 us
    pallas_call x1, Pallas kernels: 44.1 us -> 43.5 us  [body(): pl.pallas_call(convolve_kernel, out_shape=VMEM((2, NW, NZ, 2, 128), BF16)...]
where the time goes in v7:
time: 55.4 us; the launch traced here: 54.7 us
  Pallas kernels  54.6 us (99%)
    pallas_call x1, Pallas kernels, body(): pl.pallas_call(convolve_kernel, out_shape=VMEM((2, NW, NZ, 2, 128), BF16)...  43.5 us
    pallas_call x1, Pallas kernels, body(): pl.pallas_call(mix_kernel, out_shape=(VMEM((4, 256, 256), BF16), VMEM((10...  10 us
    pallas_call x1, Pallas kernels, body(): pl.pallas_call(output_kernel, out_shape=jax.ShapeDtypeStruct((256, 512),...  1.17 us

profile of v7, /device:TPU:1, one launch (start us, length us, event | category | flops | bytes accessed | tf_op | source)
XLA Modules:
  0.0 54.7 jit_solution(18397737157531409840)
XLA Ops:
  0.0 43.5 %shard_map.55.back = bf16[2,8,16,2,128]{4,3,2,1,0:T(2,128)(2,1)S(1)} custom-call(f32[256,256]{1,0:T(8,128)} %values_hbm.3, f32[32,256]{1,0:T(8,128)} %taps_hbm.1), custom_call_target="tpu_custom_call" | custom-call | tf_op jit(solution)/shard_map/pallas_call | solution.py:281
  43.5 10.0 %shard_map.56 = (bf16[4,256,256]{2,1,0:T(8,128)(2,1)S(1)}, bf16[1024,512]{1,0:T(8,128)(2,1)S(1)}) custom-call(bf16[2,8,16,2,128]{4,3,2,1,0:T(2,128)(2,1)S(1)} %shard_map.55.back, f32[256,256]{1,0:T(8,128)} %values_hbm.3, f32[256,256]{1,0:T(8,128)} %gates_hbm.1, f32[1,256]{1,0:T(1,128)} %bitcast.1, bf16[1024,512]{1,0:T(8,128)(2,1)} %weight_hbm.1), custom_call_target="tpu_custom_call" | custom-call | tf_op jit(solution)/shard_map/pallas_call | solution.py:296
  53.5 1.2 %shard_map.57 = f32[256,512]{1,0:T(8,128)} custom-call(bf16[4,256,256]{2,1,0:T(8,128)(2,1)S(1)} %get-tuple-element.7.gathered, bf16[1024,512]{1,0:T(8,128)(2,1)S(1)} %get-tuple-element.8.weight), custom_call_target="tpu_custom_call" | custom-call | tf_op jit(solution)/shard_map/pallas_call | solution.py:307

commit v8 on v7

--- a/solution.py
+++ b/solution.py
@@ -207,7 +207,6 @@
         load.start()
     loads[0].wait()
     loads[1].wait()
-    wait_for(2)
 
     def piece(slot, quarter):
         return gathered.at[slot, pl.ds(64 * quarter, 64)]
@@ -235,12 +234,10 @@
             [arrived[32 * w + 8 * q:32 * w + 8 * q + 8] for q in range(4) for w in range(NW)], axis=0).T
         hidden = (gates[rows, :] * (convolved + skip_ref[...] * values[rows, :])).astype(BF16)
         gathered[my_ch, rows, :] = hidden
-        for quarter in (2 * half, 2 * half + 1):
-            (to_left if half else to_right)(quarter).start()
-    for quarter in (2, 3):
-        to_right(quarter).start()
-    for quarter in (0, 1):
-        to_left(quarter).start()
+    wait_for(2)
+    for right_one, left_one in ((0, 2), (1, 3), (2, 0), (3, 1)):
+        to_right(right_one).start()
+        to_left(left_one).start()
     for first, second in ((0, 2), (1, 3)):
         to_right(first).wait_recv()
         pass_on(first).start()

time: 55.4 us -> 55.2 us (level)
  no operation moved by 1% of the time
where the time goes in v8:
time: 55.2 us; the launch traced here: 54.9 us
  Pallas kernels  54.9 us (99%)
    pallas_call x1, Pallas kernels, body(): pl.pallas_call(convolve_kernel, out_shape=VMEM((2, NW, NZ, 2, 128), BF16)...  43.5 us
    pallas_call x1, Pallas kernels, body(): pl.pallas_call(mix_kernel, out_shape=(VMEM((4, 256, 256), BF16), VMEM((10...  10.3 us
    pallas_call x1, Pallas kernels, body(): pl.pallas_call(output_kernel, out_shape=jax.ShapeDtypeStruct((256, 512),...  1.16 us

profile of v8, /device:TPU:1, one launch (start us, length us, event | category | flops | bytes accessed | tf_op | source)
XLA Modules:
  0.0 54.9 jit_solution(7427525972457840499)
XLA Ops:
  0.0 43.5 %shard_map.55.back = bf16[2,8,16,2,128]{4,3,2,1,0:T(2,128)(2,1)S(1)} custom-call(f32[256,256]{1,0:T(8,128)} %values_hbm.3, f32[32,256]{1,0:T(8,128)} %taps_hbm.1), custom_call_target="tpu_custom_call" | custom-call | tf_op jit(solution)/shard_map/pallas_call | solution.py:278
  43.5 10.3 %shard_map.56 = (bf16[4,256,256]{2,1,0:T(8,128)(2,1)S(1)}, bf16[1024,512]{1,0:T(8,128)(2,1)S(1)}) custom-call(bf16[2,8,16,2,128]{4,3,2,1,0:T(2,128)(2,1)S(1)} %shard_map.55.back, f32[256,256]{1,0:T(8,128)} %values_hbm.3, f32[256,256]{1,0:T(8,128)} %gates_hbm.1, f32[1,256]{1,0:T(1,128)} %bitcast.1, bf16[1024,512]{1,0:T(8,128)(2,1)} %weight_hbm.1), custom_call_target="tpu_custom_call" | custom-call | tf_op jit(solution)/shard_map/pallas_call | solution.py:293
  53.8 1.2 %shard_map.57 = f32[256,512]{1,0:T(8,128)} custom-call(bf16[4,256,256]{2,1,0:T(8,128)(2,1)S(1)} %get-tuple-element.7.gathered, bf16[1024,512]{1,0:T(8,128)(2,1)S(1)} %get-tuple-element.8.weight), custom_call_target="tpu_custom_call" | custom-call | tf_op jit(solution)/shard_map/pallas_call | solution.py:304
